TPU v7x, 32 devices: a whole 2x2x4 slice. The times are simulated.
32 devices in a mesh: fsdp: 16 (over z, x, core), tp: 2 (over y).
Axes of the slice: x: 2, y: 2, z: 4, core: 2. Of those that a mesh axis runs over, the one named last changes fastest.
Arguments:
- inputs: bfloat16 [32768, 1024], P(('fsdp', 'tp')), may hold values from -6 to 6
- cotangent: bfloat16 [32768, 1024], P(('fsdp', 'tp')), may hold values from -18 to 18
- first_gain: float32 [1024], replicated, may hold values from 0.5 to 1.5
- first_shift: float32 [1024], replicated, may hold values from -1.5 to 1.5
- second_gain: float32 [1024], replicated, may hold values from 0.5 to 1.5
- second_shift: float32 [1024], replicated, may hold values from -1.5 to 1.5
- project_weight: bfloat16 [1024, 3, 1024], P('fsdp', None, 'tp'), may hold values from -0.1875 to 0.1875
- project_bias: float32 [3, 1024], P(None, 'tp'), may hold values from -1.5 to 1.5
- dense_weight: bfloat16 [1024, 1024], P('tp', 'fsdp'), may hold values from -4 to 4
- dense_bias: float32 [1024], replicated, may hold values from -1.5 to 1.5
- expand_weight: bfloat16 [1024, 4096], P('fsdp', 'tp'), may hold values from -0.1875 to 0.1875
- expand_bias: float32 [4096], P('tp'), may hold values from -2.5 to 2.5
- shrink_weight: bfloat16 [4096, 1024], P('tp', 'fsdp'), may hold values from -0.09375 to 0.09375
- shrink_bias: float32 [1024], replicated, may hold values from -1.5 to 1.5
Outputs:
- output: bfloat16 [32768, 1024], P(('fsdp', 'tp'))
- input_grad: float32 [32768, 1024], P(('fsdp', 'tp'))
- first_gain_grad: float32 [1024], replicated
- first_shift_grad: float32 [1024], replicated
- second_gain_grad: float32 [1024], replicated
- second_shift_grad: float32 [1024], replicated
- project_weight_grad: float32 [1024, 3, 1024], P('fsdp', None, 'tp')
- project_bias_grad: float32 [3, 1024], P(None, 'tp')
- dense_weight_grad: float32 [1024, 1024], P('tp', 'fsdp')
- dense_bias_grad: float32 [1024], replicated
- expand_weight_grad: float32 [1024, 4096], P('fsdp', 'tp')
- expand_bias_grad: float32 [4096], P('tp')
- shrink_weight_grad: float32 [4096, 1024], P('tp', 'fsdp')
- shrink_bias_grad: float32 [1024], replicated
All inputs are finite; a program needn't handle non-finite values.
Results may differ from a plain program's by a relative error of at most 0.0094.
Values may be sent and summed in bfloat16 or wider, within the bound.
A program may use at most 320 MiB of HBM per device.

v0:
```python
import jax
import jax.numpy as jnp
from jax import lax
from jax.sharding import PartitionSpec as P

HS = 64
ROT = 16
LEN = 2048
EPS = 1e-05


def normalize(values, gain_vector, shift_vector):
    mean_row = jnp.mean(values, axis=-1, keepdims=True)
    centred = values - mean_row
    spread = lax.rsqrt(jnp.mean(centred * centred, axis=-1, keepdims=True) + EPS)
    normal = centred * spread
    return (normal * gain_vector + shift_vector, normal, spread)


def norm_back(grad_in, normal, spread, gain_vector):
    scaled = grad_in * gain_vector
    mean_first = jnp.mean(scaled, axis=-1, keepdims=True)
    mean_second = jnp.mean(scaled * normal, axis=-1, keepdims=True)
    return spread * (scaled - mean_first - normal * mean_second)


def rotary_tables(row_count):
    half_rot = ROT // 2
    position = (jnp.arange(row_count) % LEN).astype(jnp.float32)
    inverse = 10000.0 ** (-(jnp.arange(half_rot).astype(jnp.float32) * 2.0) / ROT)
    angle = position[:, None] * inverse[None, :]
    return (jnp.cos(angle), jnp.sin(angle))


def rotate(heads_in, cosine_table, sine_table):
    half_rot = ROT // 2
    first_half = heads_in[..., :half_rot]
    second_half = heads_in[..., half_rot:ROT]
    cos_wide = cosine_table[:, None, :]
    sin_wide = sine_table[:, None, :]
    return jnp.concatenate(
        [
            first_half * cos_wide - second_half * sin_wide,
            second_half * cos_wide + first_half * sin_wide,
            heads_in[..., ROT:],
        ],
        axis=-1,
    )


def causal_scores(query_rows, key_rows, first_row, score_scale):
    block_rows = query_rows.shape[0]
    raw_scores = (
        jnp.einsum("qhd,khd->hqk", query_rows, key_rows, preferred_element_type=jnp.float32)
        * score_scale
    )
    row_pos = first_row + jnp.arange(block_rows)[:, None]
    col_pos = jnp.arange(key_rows.shape[0])[None, :]
    return jnp.where((col_pos <= row_pos)[None], raw_scores, -1e30)


def gelu_exact(pre_act):
    return jax.nn.gelu(pre_act, approximate=False)


def body(
    inputs,
    cotangent,
    first_gain,
    first_shift,
    second_gain,
    second_shift,
    project_weight,
    project_bias,
    dense_weight,
    dense_bias,
    expand_weight,
    expand_bias,
    shrink_weight,
    shrink_bias,
):
    project_full, expand_full = (
        lax.all_gather(project_weight, "fsdp", axis=0, tiled=True),
        lax.all_gather(expand_weight, "fsdp", axis=0, tiled=True),
    )
    dense_full, shrink_full = (
        lax.all_gather(dense_weight, "fsdp", axis=1, tiled=True),
        lax.all_gather(shrink_weight, "fsdp", axis=1, tiled=True),
    )
    model_width = project_full.shape[0]
    local_width = project_full.shape[2]
    heads_here = local_width // HS
    own_rows = inputs.astype(jnp.float32)
    own_grads = cotangent.astype(jnp.float32)
    first_out, first_normal, first_spread = normalize(own_rows, first_gain, first_shift)
    second_out, second_normal, second_spread = normalize(own_rows, second_gain, second_shift)
    first_normed, second_normed = (
        lax.all_gather(first_out.astype(jnp.bfloat16), "tp", axis=0, tiled=True),
        lax.all_gather(second_out.astype(jnp.bfloat16), "tp", axis=0, tiled=True),
    )
    row_count = first_normed.shape[0]
    seq_count = row_count // LEN
    block_rows = min(512, LEN)
    block_count = LEN // block_rows
    score_scale = HS ** (-0.5)
    project_flat = project_full.reshape(model_width, 3 * local_width)
    joined_rows = (
        jnp.dot(first_normed, project_flat, preferred_element_type=jnp.float32).reshape(
            row_count, 3, local_width
        )
        + project_bias[None]
    )
    cosine_table, sine_table = rotary_tables(row_count)
    queries = rotate(
        joined_rows[:, 0].reshape(row_count, heads_here, HS), cosine_table, sine_table
    ).astype(jnp.bfloat16)
    keys_all = rotate(
        joined_rows[:, 1].reshape(row_count, heads_here, HS), cosine_table, sine_table
    ).astype(jnp.bfloat16)
    values_all = joined_rows[:, 2].reshape(row_count, heads_here, HS).astype(jnp.bfloat16)

    def attend_sequence(seq_index):
        seq_start = seq_index * LEN
        seq_keys = lax.dynamic_slice_in_dim(keys_all, seq_start, LEN, 0)
        seq_values = lax.dynamic_slice_in_dim(values_all, seq_start, LEN, 0)

        def attend_block(block_index):
            first_row = block_index * block_rows
            block_queries = lax.dynamic_slice_in_dim(queries, seq_start + first_row, block_rows, 0)
            scores = causal_scores(block_queries, seq_keys, first_row, score_scale)
            row_top = jnp.max(scores, axis=-1, keepdims=True)
            shifted = jnp.exp(scores - row_top)
            row_total = jnp.sum(shifted, axis=-1, keepdims=True)
            weights_low = (shifted / row_total).astype(jnp.bfloat16)
            mixture = jnp.einsum(
                "hqk,khd->qhd", weights_low, seq_values, preferred_element_type=jnp.float32
            )
            return (mixture.astype(jnp.bfloat16), (row_top + jnp.log(row_total))[..., 0])

        return lax.map(attend_block, jnp.arange(block_count))

    context_blocks, log_totals = lax.map(attend_sequence, jnp.arange(seq_count))
    context = context_blocks.reshape(row_count, local_width)
    pre_act = jnp.dot(second_normed, expand_full, preferred_element_type=jnp.float32) + expand_bias
    activation = gelu_exact(pre_act).astype(jnp.bfloat16)
    branch = lax.psum_scatter(
        jnp.dot(context, dense_full, preferred_element_type=jnp.float32)
        + jnp.dot(activation, shrink_full, preferred_element_type=jnp.float32),
        "tp",
        scatter_dimension=0,
        tiled=True,
    )
    output = (own_rows + branch + dense_bias + shrink_bias).astype(jnp.bfloat16)
    grad_rows = lax.all_gather(cotangent, "tp", axis=0, tiled=True)
    dense_grad = jnp.dot(context.T, grad_rows, preferred_element_type=jnp.float32)
    shrink_grad = jnp.dot(activation.T, grad_rows, preferred_element_type=jnp.float32)
    context_grad = jnp.dot(grad_rows, dense_full.T, preferred_element_type=jnp.float32).astype(
        jnp.bfloat16
    )
    activation_grad = jnp.dot(grad_rows, shrink_full.T, preferred_element_type=jnp.float32)
    unused_value, gelu_pull = jax.vjp(gelu_exact, pre_act)
    pre_grad = gelu_pull(activation_grad)[0].astype(jnp.bfloat16)
    expand_grad = jnp.dot(second_normed.T, pre_grad, preferred_element_type=jnp.float32)
    expand_bias_part = jnp.sum(pre_grad.astype(jnp.float32), axis=0)
    second_grad = jnp.dot(pre_grad, expand_full.T, preferred_element_type=jnp.float32)
    context_heads = context_grad.reshape(row_count, heads_here, HS)

    def back_sequence(pack):
        seq_index, seq_totals = pack
        seq_start = seq_index * LEN
        seq_keys = lax.dynamic_slice_in_dim(keys_all, seq_start, LEN, 0)
        seq_values = lax.dynamic_slice_in_dim(values_all, seq_start, LEN, 0)

        def back_block(carry, item):
            key_sum, value_sum = carry
            block_index, block_totals = item
            first_row = block_index * block_rows
            block_queries = lax.dynamic_slice_in_dim(queries, seq_start + first_row, block_rows, 0)
            block_grads = lax.dynamic_slice_in_dim(
                context_heads, seq_start + first_row, block_rows, 0
            )
            scores = causal_scores(block_queries, seq_keys, first_row, score_scale)
            attention = jnp.exp(scores - block_totals[..., None])
            prob_grad = jnp.einsum(
                "qhd,khd->hqk", block_grads, seq_values, preferred_element_type=jnp.float32
            )
            score_grad = (
                attention * (prob_grad - jnp.sum(attention * prob_grad, axis=-1, keepdims=True))
            ).astype(jnp.bfloat16)
            query_part = (
                jnp.einsum("hqk,khd->qhd", score_grad, seq_keys, preferred_element_type=jnp.float32)
                * score_scale
            )
            key_sum = (
                key_sum
                + jnp.einsum(
                    "hqk,qhd->khd", score_grad, block_queries, preferred_element_type=jnp.float32
                )
                * score_scale
            )
            value_sum = value_sum + jnp.einsum(
                "hqk,qhd->khd",
                attention.astype(jnp.bfloat16),
                block_grads,
                preferred_element_type=jnp.float32,
            )
            return ((key_sum, value_sum), query_part)

        zero_heads = jnp.zeros((LEN, heads_here, HS), jnp.float32)
        (key_sum, value_sum), query_parts = lax.scan(
            back_block, (zero_heads, zero_heads), (jnp.arange(block_count), seq_totals)
        )
        return (query_parts.reshape(LEN, heads_here, HS), key_sum, value_sum)

    query_grad, key_grad, value_grad = lax.map(back_sequence, (jnp.arange(seq_count), log_totals))
    query_grad = rotate(query_grad.reshape(row_count, heads_here, HS), cosine_table, -sine_table)
    key_grad = rotate(key_grad.reshape(row_count, heads_here, HS), cosine_table, -sine_table)
    joined_grad = jnp.stack(
        [
            query_grad.reshape(row_count, local_width),
            key_grad.reshape(row_count, local_width),
            value_grad.reshape(row_count, local_width),
        ],
        axis=1,
    ).astype(jnp.bfloat16)
    project_bias_part = jnp.sum(joined_grad.astype(jnp.float32), axis=0)
    joined_flat = joined_grad.reshape(row_count, 3 * local_width)
    project_grad = jnp.dot(first_normed.T, joined_flat, preferred_element_type=jnp.float32).reshape(
        model_width, 3, local_width
    )
    first_grad = jnp.dot(joined_flat, project_flat.T, preferred_element_type=jnp.float32)
    first_rows, second_rows = (
        lax.psum_scatter(first_grad, "tp", scatter_dimension=0, tiled=True),
        lax.psum_scatter(second_grad, "tp", scatter_dimension=0, tiled=True),
    )
    input_grad = (
        own_grads
        + norm_back(first_rows, first_normal, first_spread, first_gain)
        + norm_back(second_rows, second_normal, second_spread, second_gain)
    )
    first_gain_part = jnp.sum(first_rows * first_normal, axis=0)
    first_shift_part = jnp.sum(first_rows, axis=0)
    second_gain_part = jnp.sum(second_rows * second_normal, axis=0)
    second_shift_part = jnp.sum(second_rows, axis=0)
    out_bias_part = jnp.sum(own_grads, axis=0)
    first_gain_grad, first_shift_grad, second_gain_grad, second_shift_grad, out_bias_grad = (
        lax.psum(
            (first_gain_part, first_shift_part, second_gain_part, second_shift_part, out_bias_part),
            ("fsdp", "tp"),
        )
    )
    project_bias_grad, expand_bias_grad = lax.psum((project_bias_part, expand_bias_part), "fsdp")
    project_weight_grad, expand_weight_grad = (
        lax.psum_scatter(project_grad, "fsdp", scatter_dimension=0, tiled=True),
        lax.psum_scatter(expand_grad, "fsdp", scatter_dimension=0, tiled=True),
    )
    dense_weight_grad, shrink_weight_grad = (
        lax.psum_scatter(dense_grad, "fsdp", scatter_dimension=1, tiled=True),
        lax.psum_scatter(shrink_grad, "fsdp", scatter_dimension=1, tiled=True),
    )
    return (
        output,
        input_grad,
        first_gain_grad,
        first_shift_grad,
        second_gain_grad,
        second_shift_grad,
        project_weight_grad,
        project_bias_grad,
        dense_weight_grad,
        out_bias_grad,
        expand_weight_grad,
        expand_bias_grad,
        shrink_weight_grad,
        out_bias_grad,
    )


def solution(mesh):
    return jax.shard_map(
        body,
        mesh=mesh,
        in_specs=(
            P(("fsdp", "tp"), None),
            P(("fsdp", "tp"), None),
            P(),
            P(),
            P(),
            P(),
            P("fsdp", None, "tp"),
            P(None, "tp"),
            P("tp", "fsdp"),
            P(),
            P("fsdp", "tp"),
            P("tp"),
            P("tp", "fsdp"),
            P(),
        ),
        out_specs=(
            P(("fsdp", "tp"), None),
            P(("fsdp", "tp"), None),
            P(),
            P(),
            P(),
            P(),
            P("fsdp", None, "tp"),
            P(None, "tp"),
            P("tp", "fsdp"),
            P(),
            P("fsdp", "tp"),
            P("tp"),
            P("tp", "fsdp"),
            P(),
        ),
        check_vma=False,
    )
```

profile of v0, /device:TPU:0, one launch (start us, length us, event | category | flops | bytes accessed | tf_op | source)
XLA Modules:
  0.0 1660.7 jit_solution(12958320723334942280)
XLA Ops:
  18.0 32.8 %all-gather.12.cloned.1.call-done = bf16[512,1024]{0,1:T(8,128)(2,1)} async-done(((bf16[512,64]{0,1:T(8,128)(2,1)}), bf16[512,1024]{0,1:T(8,128)(2,1)}) %all-gather.12.cloned.1.call-update) | async-done | bytes 1048592 | tf_op jit(solution)/shard_map/all_gather | solution.py:87
  50.8 57.3 %all-gather.20.cloned.1.call-done = bf16[2048,1024]{1,0:T(8,128)(2,1)} async-done(((bf16[1024,1024]{1,0:T(8,128)(2,1)}), bf16[2048,1024]{1,0:T(8,128)(2,1)}) %all-gather.20.cloned.1.call-update) | async-done | bytes 4194320 | tf_op jit(solution)/shard_map/all_gather | solution.py:154
  114.3 41.5 %all-gather.10.cloned.1.call-done = bf16[1024,3,512]{2,0,1:T(8,128)(2,1)} async-done(((bf16[64,3,512]{2,0,1:T(8,128)(2,1)}), bf16[1024,3,512]{2,0,1:T(8,128)(2,1)}) %all-gather.10.cloned.1.call-update) | async-done | bytes 3145744 | tf_op jit(solution)/shard_map/all_gather | solution.py:83
  160.5 51.8 %all-gather.8.cloned.1.call-done = bf16[2048,1024]{1,0:T(8,128)(2,1)} async-done(((bf16[1024,1024]{1,0:T(8,128)(2,1)}), bf16[2048,1024]{1,0:T(8,128)(2,1)}) %all-gather.8.cloned.1.call-update) | async-done | bytes 4194320 | tf_op jit(solution)/shard_map/all_gather | solution.py:98
  227.0 191.0 %while.49 = (s32[]{:T(128)}, bf16[4,512,8,64]{1,3,2,0:T(8,128)(2,1)}, f32[4,8,512]{2,1,0:T(8,128)S(1)}, s32[4]{0:T(128)S(1)}, bf16[2048,8,64]{0,2,1:T(8,128)(2,1...) while((s32[]{:T(128)}, ...), condition=%wide.region_5.6_spmd, body=%wide.region_2.5_spmd.sunk | while | flops 2249454080 | bytes 110236336 | solution.py:140
  229.4 14.8 fusion.120
  244.3 15.0 fusion.121
  259.3 15.6 fusion.122
  276.8 14.9 fusion.120
  291.7 15.3 fusion.121
  307.0 15.7 fusion.122
  324.6 15.0 fusion.120
  339.6 15.2 fusion.121
  354.8 15.8 fusion.122
  372.6 14.8 fusion.120
  387.4 15.0 fusion.121
  402.4 15.6 fusion.122
  418.0 523.5 %while.50 = (s32[]{:T(128)}, f32[2048,8,64]{0,2,1:T(8,128)}, f32[2048,8,64]{0,2,1:T(8,128)}, f32[4,512,8,64]{1,0,3,2:T(4,128)}, s32[4]{0:T(128)S(1)}, /*index=5*...) while((s32[]{:T(128)}, f32[2048,8,64]{0,2,1:T(8,128)}, ...), condition=%wide.region_9.10_spmd.clone, body=%wide.region_7.9_spmd.clone.sunk | while | flops 5450756608 | bytes 284250304 | solution.py:210
  419.4 17.4 %fusion.132 = f32[8,512,2048]{2,1,0:T(8,128)} fusion(bf16[2048,8,64]{0,2,1:T(8,128)(2,1)} %get-tuple-element.520, bf16[2048,8,64]{0,2,1:T(8,128)(2,1)} %get-tuple-element.519, s32[]{:T(128)S(6)} %select_n.101), kind=kOutput, calls=%fused_computation.28.clone.1 | convolution fusion | flops 1073741824 | bytes 36175876 | tf_op jit(solution)/shard_map/while/body/eval_jaxpr/while/body/eval_jaxpr/qhd,khd->hqk/dot_general | solution.py:184
  437.4 24.6 %multiply_reduce_fusion.4 = (f32[8,512]{1,0:T(8,128)S(1)}, f32[8,512,2048]{2,1,0:T(8,128)}) fusion(f32[8,512,2048]{2,1,0:T(8,128)} %fusion.132, f32[8,512]{1,0:T(8,128)S(1)} %dynamic-slice_bitcast_fusion.2, bf16[2048,8,64]{0,2,1:T(8,128)(2,1)S(1)} %get-tuple-element.517, bf16[2048,8,64]{0,2,1:T(8,128)(2,1)} %get-tuple-element.516, ...), kind=kOutput, calls=%fused_computation.18.clone.1 | convolution fusion | flops 1115680768 | bytes 70811648 | tf_op jit(solution)/shard_map/while/body/eval_jaxpr/while/body/eval_jaxpr/qhd,khd->hqk/dot_general | solution.py:54
  462.1 27.4 %multiply_convert_fusion.3 = bf16[8,512,2048]{2,1,0:T(8,128)(2,1)} fusion(f32[8,512,2048]{2,1,0:T(8,128)} %get-tuple-element.448, f32[8,512,2048]{2,1,0:T(8,128)} %fusion.132, f32[8,512]{1,0:T(8,128)S(1)} %get-tuple-element.449), kind=kLoop, calls=%fused_computation.17.clone.1 | loop fusion | flops 25165824 | bytes 83902464 | tf_op jit(solution)/shard_map/while/body/eval_jaxpr/while/body/eval_jaxpr/convert_element_type | solution.py:189
  499.3 21.0 %dynamic_update_slice.39 = f32[4,512,8,64]{1,0,3,2:T(4,128)} dynamic-update-slice(f32[4,512,8,64]{1,0,3,2:T(4,128)} %get-tuple-element.500, f32[1,512,8,64]{1,0,3,2:T(1,128)S(1)} %copy.59, s32[]{:T(128)} %get-tuple-element.497, s32[]{:T(128)} %constant.176.clone.1..sunk.1, s32[]{:T(128)} %constant.176.clone.1..sunk.1, s32[]{:T(128)} %constant.176.clone.1..sunk.1) | dynamic-update-slice | bytes 2097156 | tf_op jit(solution)/shard_map/while/body/eval_jaxpr/while/body/jit(dynamic_update_index_in_dim)/dynamic_update_slice | solution.py:210
  531.3 15.8 bitcast_add_fusion.5
  548.3 17.4 %fusion.132 = f32[8,512,2048]{2,1,0:T(8,128)} fusion(bf16[2048,8,64]{0,2,1:T(8,128)(2,1)} %get-tuple-element.520, bf16[2048,8,64]{0,2,1:T(8,128)(2,1)} %get-tuple-element.519, s32[]{:T(128)S(6)} %select_n.101), kind=kOutput, calls=%fused_computation.28.clone.1 | convolution fusion | flops 1073741824 | bytes 36175876 | tf_op jit(solution)/shard_map/while/body/eval_jaxpr/while/body/eval_jaxpr/qhd,khd->hqk/dot_general | solution.py:184
  566.4 24.6 %multiply_reduce_fusion.4 = (f32[8,512]{1,0:T(8,128)S(1)}, f32[8,512,2048]{2,1,0:T(8,128)}) fusion(f32[8,512,2048]{2,1,0:T(8,128)} %fusion.132, f32[8,512]{1,0:T(8,128)S(1)} %dynamic-slice_bitcast_fusion.2, bf16[2048,8,64]{0,2,1:T(8,128)(2,1)S(1)} %get-tuple-element.517, bf16[2048,8,64]{0,2,1:T(8,128)(2,1)} %get-tuple-element.516, ...), kind=kOutput, calls=%fused_computation.18.clone.1 | convolution fusion | flops 1115680768 | bytes 70811648 | tf_op jit(solution)/shard_map/while/body/eval_jaxpr/while/body/eval_jaxpr/qhd,khd->hqk/dot_general | solution.py:54
  591.0 27.4 %multiply_convert_fusion.3 = bf16[8,512,2048]{2,1,0:T(8,128)(2,1)} fusion(f32[8,512,2048]{2,1,0:T(8,128)} %get-tuple-element.448, f32[8,512,2048]{2,1,0:T(8,128)} %fusion.132, f32[8,512]{1,0:T(8,128)S(1)} %get-tuple-element.449), kind=kLoop, calls=%fused_computation.17.clone.1 | loop fusion | flops 25165824 | bytes 83902464 | tf_op jit(solution)/shard_map/while/body/eval_jaxpr/while/body/eval_jaxpr/convert_element_type | solution.py:189
  628.2 21.0 %dynamic_update_slice.39 = f32[4,512,8,64]{1,0,3,2:T(4,128)} dynamic-update-slice(f32[4,512,8,64]{1,0,3,2:T(4,128)} %get-tuple-element.500, f32[1,512,8,64]{1,0,3,2:T(1,128)S(1)} %copy.59, s32[]{:T(128)} %get-tuple-element.497, s32[]{:T(128)} %constant.176.clone.1..sunk.1, s32[]{:T(128)} %constant.176.clone.1..sunk.1, s32[]{:T(128)} %constant.176.clone.1..sunk.1) | dynamic-update-slice | bytes 2097156 | tf_op jit(solution)/shard_map/while/body/eval_jaxpr/while/body/jit(dynamic_update_index_in_dim)/dynamic_update_slice | solution.py:210
  661.4 17.0 %bitcast_add_fusion.5 = f32[2048,8,64]{0,2,1:T(8,128)} fusion(f32[2048,8,64]{0,2,1:T(8,128)} %get-tuple-element.499, f32[8,512,2048]{2,1,0:T(8,128)} %get-tuple-element.448, pred[]{:T(512)S(6)} %compare.4, bf16[2048,8,64]{0,2,1:T(8,128)(2,1)} %get-tuple-element.519, s32[]{:T(128)S(6)} %select_n.101), kind=kOutput, calls=%fused_computation.22.clone.1 | convolution fusion | flops 1084227584 | bytes 42467332 | tf_op jit(solution)/shard_map/while/body/eval_jaxpr/while/body/eval_jaxpr/hqk,qhd->khd/dot_general | solution.py:201
  679.7 17.4 %fusion.132 = f32[8,512,2048]{2,1,0:T(8,128)} fusion(bf16[2048,8,64]{0,2,1:T(8,128)(2,1)} %get-tuple-element.520, bf16[2048,8,64]{0,2,1:T(8,128)(2,1)} %get-tuple-element.519, s32[]{:T(128)S(6)} %select_n.101), kind=kOutput, calls=%fused_computation.28.clone.1 | convolution fusion | flops 1073741824 | bytes 36175876 | tf_op jit(solution)/shard_map/while/body/eval_jaxpr/while/body/eval_jaxpr/qhd,khd->hqk/dot_general | solution.py:184
  697.7 24.6 %multiply_reduce_fusion.4 = (f32[8,512]{1,0:T(8,128)S(1)}, f32[8,512,2048]{2,1,0:T(8,128)}) fusion(f32[8,512,2048]{2,1,0:T(8,128)} %fusion.132, f32[8,512]{1,0:T(8,128)S(1)} %dynamic-slice_bitcast_fusion.2, bf16[2048,8,64]{0,2,1:T(8,128)(2,1)S(1)} %get-tuple-element.517, bf16[2048,8,64]{0,2,1:T(8,128)(2,1)} %get-tuple-element.516, ...), kind=kOutput, calls=%fused_computation.18.clone.1 | convolution fusion | flops 1115680768 | bytes 70811648 | tf_op jit(solution)/shard_map/while/body/eval_jaxpr/while/body/eval_jaxpr/qhd,khd->hqk/dot_general | solution.py:54
  722.3 27.4 %multiply_convert_fusion.3 = bf16[8,512,2048]{2,1,0:T(8,128)(2,1)} fusion(f32[8,512,2048]{2,1,0:T(8,128)} %get-tuple-element.448, f32[8,512,2048]{2,1,0:T(8,128)} %fusion.132, f32[8,512]{1,0:T(8,128)S(1)} %get-tuple-element.449), kind=kLoop, calls=%fused_computation.17.clone.1 | loop fusion | flops 25165824 | bytes 83902464 | tf_op jit(solution)/shard_map/while/body/eval_jaxpr/while/body/eval_jaxpr/convert_element_type | solution.py:189
  759.6 21.0 %dynamic_update_slice.39 = f32[4,512,8,64]{1,0,3,2:T(4,128)} dynamic-update-slice(f32[4,512,8,64]{1,0,3,2:T(4,128)} %get-tuple-element.500, f32[1,512,8,64]{1,0,3,2:T(1,128)S(1)} %copy.59, s32[]{:T(128)} %get-tuple-element.497, s32[]{:T(128)} %constant.176.clone.1..sunk.1, s32[]{:T(128)} %constant.176.clone.1..sunk.1, s32[]{:T(128)} %constant.176.clone.1..sunk.1) | dynamic-update-slice | bytes 2097156 | tf_op jit(solution)/shard_map/while/body/eval_jaxpr/while/body/jit(dynamic_update_index_in_dim)/dynamic_update_slice | solution.py:210
  792.8 17.0 %bitcast_add_fusion.5 = f32[2048,8,64]{0,2,1:T(8,128)} fusion(f32[2048,8,64]{0,2,1:T(8,128)} %get-tuple-element.499, f32[8,512,2048]{2,1,0:T(8,128)} %get-tuple-element.448, pred[]{:T(512)S(6)} %compare.4, bf16[2048,8,64]{0,2,1:T(8,128)(2,1)} %get-tuple-element.519, s32[]{:T(128)S(6)} %select_n.101), kind=kOutput, calls=%fused_computation.22.clone.1 | convolution fusion | flops 1084227584 | bytes 42467332 | tf_op jit(solution)/shard_map/while/body/eval_jaxpr/while/body/eval_jaxpr/hqk,qhd->khd/dot_general | solution.py:201
  811.0 17.4 %fusion.132 = f32[8,512,2048]{2,1,0:T(8,128)} fusion(bf16[2048,8,64]{0,2,1:T(8,128)(2,1)} %get-tuple-element.520, bf16[2048,8,64]{0,2,1:T(8,128)(2,1)} %get-tuple-element.519, s32[]{:T(128)S(6)} %select_n.101), kind=kOutput, calls=%fused_computation.28.clone.1 | convolution fusion | flops 1073741824 | bytes 36175876 | tf_op jit(solution)/shard_map/while/body/eval_jaxpr/while/body/eval_jaxpr/qhd,khd->hqk/dot_general | solution.py:184
  829.0 24.6 %multiply_reduce_fusion.4 = (f32[8,512]{1,0:T(8,128)S(1)}, f32[8,512,2048]{2,1,0:T(8,128)}) fusion(f32[8,512,2048]{2,1,0:T(8,128)} %fusion.132, f32[8,512]{1,0:T(8,128)S(1)} %dynamic-slice_bitcast_fusion.2, bf16[2048,8,64]{0,2,1:T(8,128)(2,1)S(1)} %get-tuple-element.517, bf16[2048,8,64]{0,2,1:T(8,128)(2,1)} %get-tuple-element.516, ...), kind=kOutput, calls=%fused_computation.18.clone.1 | convolution fusion | flops 1115680768 | bytes 70811648 | tf_op jit(solution)/shard_map/while/body/eval_jaxpr/while/body/eval_jaxpr/qhd,khd->hqk/dot_general | solution.py:54
  853.7 27.4 %multiply_convert_fusion.3 = bf16[8,512,2048]{2,1,0:T(8,128)(2,1)} fusion(f32[8,512,2048]{2,1,0:T(8,128)} %get-tuple-element.448, f32[8,512,2048]{2,1,0:T(8,128)} %fusion.132, f32[8,512]{1,0:T(8,128)S(1)} %get-tuple-element.449), kind=kLoop, calls=%fused_computation.17.clone.1 | loop fusion | flops 25165824 | bytes 83902464 | tf_op jit(solution)/shard_map/while/body/eval_jaxpr/while/body/eval_jaxpr/convert_element_type | solution.py:189
  890.9 21.0 %dynamic_update_slice.39 = f32[4,512,8,64]{1,0,3,2:T(4,128)} dynamic-update-slice(f32[4,512,8,64]{1,0,3,2:T(4,128)} %get-tuple-element.500, f32[1,512,8,64]{1,0,3,2:T(1,128)S(1)} %copy.59, s32[]{:T(128)} %get-tuple-element.497, s32[]{:T(128)} %constant.176.clone.1..sunk.1, s32[]{:T(128)} %constant.176.clone.1..sunk.1, s32[]{:T(128)} %constant.176.clone.1..sunk.1) | dynamic-update-slice | bytes 2097156 | tf_op jit(solution)/shard_map/while/body/eval_jaxpr/while/body/jit(dynamic_update_index_in_dim)/dynamic_update_slice | solution.py:210
  924.1 17.0 %bitcast_add_fusion.5 = f32[2048,8,64]{0,2,1:T(8,128)} fusion(f32[2048,8,64]{0,2,1:T(8,128)} %get-tuple-element.499, f32[8,512,2048]{2,1,0:T(8,128)} %get-tuple-element.448, pred[]{:T(512)S(6)} %compare.4, bf16[2048,8,64]{0,2,1:T(8,128)(2,1)} %get-tuple-element.519, s32[]{:T(128)S(6)} %select_n.101), kind=kOutput, calls=%fused_computation.22.clone.1 | convolution fusion | flops 1084227584 | bytes 42467332 | tf_op jit(solution)/shard_map/while/body/eval_jaxpr/while/body/eval_jaxpr/hqk,qhd->khd/dot_general | solution.py:201
  981.7 49.4 %multiply_convert_fusion.1 = (bf16[2048,2048]{1,0:T(8,128)(2,1)}, f32[2048,2048]{1,0:T(8,128)}, f32[2048,2048]{1,0:T(8,128)}) fusion(f32[2048]{0:T(1024)S(1)} %copy-done.25, bf16[2048,1024]{1,0:T(8,128)(2,1)} %all-gather.14.cloned.1.call-done, bf16[1024,2048]{1,0:T(8,128)(2,1)} %all-gather.16.cloned.1.call-done), kind=kOutput, calls=%fused_computation.42 | convolution fusion | flops 8866758656 | bytes 50339840 | tf_op jit(solution)/shard_map/dot_general | solution.py:144
  1031.0 27.8 %convert_reduce_fusion = (f32[2048]{0:T(1024)S(1)}, bf16[2048,2048]{1,0:T(8,128)(2,1)}) fusion(f32[2048,2048]{1,0:T(8,128)} %get-tuple-element.306, bf16[2048,1024]{1,0:T(8,128)(2,1)} %all-gather.20.cloned.1.call-done, bf16[2048,1024]{0,1:T(8,128)(2,1)} %all-gather.18.cloned.1.call-done, f32[2048,2048]{1,0:T(8,128)} %get-tuple-element.333, ...), kind=kOutput, calls=%fused_computation.40 | convolution fusion | flops 8661235712 | bytes 50348032 | tf_op jit(solution)/shard_map/dot_general | solution.py:160
  1136.6 14.9 fusion.74
  1152.2 61.4 %all-reduce.1 = (f32[3,512]{1,0:T(4,128)}, f32[2048]{0:T(1024)}) all-reduce(f32[3,512]{1,0:T(4,128)S(1)} %copy-done.17, f32[2048]{0:T(1024)S(1)} %get-tuple-element.334), channel_id=1, replica_groups=mesh['fsdp'=16,'tp'=2] {'fsdp'}, use_global_device_ids=true, to_apply=%region_26.27 | all-reduce | flops 3584 | bytes 28672 | tf_op jit(solution)/shard_map/psum | solution.py:252
  1219.3 64.6 %reduce-scatter.8.cloned.1.call-done = f32[1024,1024]{1,0:T(8,128)} async-done(((f32[2048,1024]{1,0:T(8,128)}), f32[1024,1024]{1,0:T(8,128)}) %reduce-scatter.8.cloned.1.call-update) | async-done | bytes 4194320 | tf_op jit(solution)/shard_map/reduce_scatter | solution.py:146
  1292.4 40.1 %all-reduce = (f32[1024]{0:T(1024)}, f32[1024]{0:T(1024)}, f32[1024]{0:T(1024)}, f32[1024]{0:T(1024)}, f32[1024]{0:T(1024)S(1)}) all-reduce(f32[1024]{0:T(1024)S(1)} %get-tuple-element.252, f32[1024]{0:T(1024)S(1)} %get-tuple-element.257, f32[1024]{0:T(1024)S(1)} %get-tuple-element.261, ...), channel_id=1, replica_groups=mesh['fsdp'=16,'tp'=2] {'fsdp','tp'}, use_global_device_ids=true, to_apply=%region_17.18 | all-reduce | flops 5120 | bytes 40960 | tf_op jit(solution)/shard_map/psum | solution.py:247
  1332.5 17.6 %reduce-scatter.16.cloned.1.call-done = f32[512,64]{0,1:T(8,128)} async-done(((f32[512,1024]{0,1:T(8,128)}), f32[512,64]{0,1:T(8,128)}) %reduce-scatter.16.cloned.1.call-update) | async-done | bytes 131088 | tf_op jit(solution)/shard_map/reduce_scatter | solution.py:258
  1350.1 88.4 %reduce-scatter.14.cloned.1.call-done = f32[64,3,512]{2,0,1:T(8,128)} async-done(((f32[1024,3,512]{2,0,1:T(8,128)}), f32[64,3,512]{2,0,1:T(8,128)}) %reduce-scatter.14.cloned.1.call-update) | async-done | bytes 393232 | tf_op jit(solution)/shard_map/reduce_scatter | solution.py:254
  1438.5 107.2 %reduce-scatter.18.cloned.1.call-done = f32[64,2048]{1,0:T(8,128)} async-done(((f32[1024,2048]{1,0:T(8,128)}), f32[64,2048]{1,0:T(8,128)}) %reduce-scatter.18.cloned.1.call-update) | async-done | bytes 524304 | tf_op jit(solution)/shard_map/reduce_scatter | solution.py:255
  1545.7 107.6 %reduce-scatter.20.cloned.1.call-done = f32[2048,64]{0,1:T(8,128)} async-done(((f32[2048,1024]{0,1:T(8,128)}), f32[2048,64]{0,1:T(8,128)}) %reduce-scatter.20.cloned.1.call-update) | async-done | bytes 524304 | tf_op jit(solution)/shard_map/reduce_scatter | solution.py:259
  (180 shorter events, 266.1 us)
Async XLA Ops:
  7.2 4.3 copy-start
  7.2 5.0 copy-start.13
  7.2 5.0 copy-start.18
  7.2 5.0 copy-start.15
  7.2 5.0 copy-start.19
  7.2 43.6 %all-gather.12.cloned.1.call-start = ((), (), s32[]{:S(2)}) async-start(), calls=%async_computation.9 | async-start | bytes 1114112 | tf_op jit(solution)/shard_map/all_gather | solution.py:87
  8.0 100.1 %all-gather.20.cloned.1.call-start = ((), (), s32[]{:S(2)}) async-start(), calls=%async_computation.14 | async-start | bytes 6291456 | tf_op jit(solution)/shard_map/all_gather | solution.py:154
  8.7 147.1 %all-gather.10.cloned.1.call-start = ((), (), s32[]{:S(2)}) async-start(), calls=%async_computation.8 | async-start | bytes 3342336 | tf_op jit(solution)/shard_map/all_gather | solution.py:83
  9.5 202.9 %all-gather.8.cloned.1.call-start = ((), (), s32[]{:S(2)}) async-start(), calls=%async_computation.7 | async-start | bytes 6291456 | tf_op jit(solution)/shard_map/all_gather | solution.py:98
  11.5 3.6 copy-start.9
  12.2 2.8 copy-start.11
  15.0 966.0 %all-gather.14.cloned.1.call-start = ((), (), s32[]{:S(2)}) async-start(), calls=%async_computation.10 | async-start | bytes 6291456 | tf_op jit(solution)/shard_map/all_gather | solution.py:99
  15.6 965.5 %all-gather.16.cloned.1.call-start = ((), (), s32[]{:S(2)}) async-start(), calls=%async_computation.11 | async-start | bytes 4456448 | tf_op jit(solution)/shard_map/all_gather | solution.py:84
  16.2 1014.8 %all-gather.18.cloned.1.call-start = ((), (), s32[]{:S(2)}) async-start(), calls=%async_computation.12 | async-start | bytes 4456448 | tf_op jit(solution)/shard_map/all_gather | solution.py:88
  17.0 1196.7 %reduce-scatter.10.cloned.1.call-start = ((), (), s32[]{:S(2)}) async-start(), calls=%async_computation.15 | async-start | bytes 12582912 | tf_op jit(solution)/shard_map/reduce_scatter | solution.py:233
  18.0 207.1 %copy-start.6 = (f32[2048,8]{0,1:T(8,128)}, f32[2048,8]{0,1:T(8,128)S(1)}, u32[]{:S(2)}) copy-start(f32[2048,8]{0,1:T(8,128)S(1)} %get-tuple-element.332) | copy-start | bytes 196612
  114.3 98.0 %copy-start.24 = (f32[3,512]{1,0:T(4,128)S(1)}, f32[3,512]{1,0:T(4,128)}, u32[]{:S(2)}) copy-start(f32[3,512]{1,0:T(4,128)} %param.25) | copy-start | bytes 18436
  947.5 5.4 copy-start.7
  947.5 5.4 copy-start.8
  964.9 7.1 copy-start.3
  969.3 2.7 copy-start.2
  981.0 0.7 copy-start.25
  981.0 232.6 %reduce-scatter.12.cloned.1.call-start = ((), (), s32[]{:S(2)}) async-start(), calls=%async_computation.16 | async-start | bytes 12582912 | tf_op jit(solution)/shard_map/reduce_scatter | solution.py:234
  1073.4 1.6 copy-start.4
  1073.4 210.5 %reduce-scatter.8.cloned.1.call-start = ((), (), s32[]{:S(2)}) async-start(), calls=%async_computation.13 | async-start | bytes 12582912 | tf_op jit(solution)/shard_map/reduce_scatter | solution.py:146
  1075.0 2.3 copy-start.23
  1077.2 11.4 copy-start.5
  1094.3 255.8 %reduce-scatter.16.cloned.1.call-start = ((), (), s32[]{:S(2)}) async-start(), calls=%async_computation.18 | async-start | bytes 2228224 | tf_op jit(solution)/shard_map/reduce_scatter | solution.py:258
  1100.3 338.2 %reduce-scatter.14.cloned.1.call-start = ((), (), s32[]{:S(2)}) async-start(), calls=%async_computation.17 | async-start | bytes 6684672 | tf_op jit(solution)/shard_map/reduce_scatter | solution.py:254
  1121.5 424.2 %reduce-scatter.18.cloned.1.call-start = ((), (), s32[]{:S(2)}) async-start(), calls=%async_computation.19 | async-start | bytes 8912896 | tf_op jit(solution)/shard_map/reduce_scatter | solution.py:255
  1136.4 517.0 %reduce-scatter.20.cloned.1.call-start = ((), (), s32[]{:S(2)}) async-start(), calls=%async_computation.20 | async-start | bytes 8912896 | tf_op jit(solution)/shard_map/reduce_scatter | solution.py:259
  1151.5 0.7 copy-start.17
  1151.5 62.1 %copy-start.1 = (bf16[1024,1024]{1,0:T(8,128)(2,1)S(1)}, bf16[1024,1024]{1,0:T(8,128)(2,1)}, u32[]{:S(2)}) copy-start(bf16[1024,1024]{1,0:T(8,128)(2,1)} %param.18) | copy-start | bytes 6291460
  1151.5 62.1 %copy-start.10 = (f32[1024]{0:T(1024)S(1)}, f32[1024]{0:T(1024)}, u32[]{:S(2)}) copy-start(f32[1024]{0:T(1024)} %copy-done.9) | copy-start | bytes 12292
  1151.5 62.1 %copy-start.12 = (f32[1024]{0:T(1024)S(1)}, f32[1024]{0:T(1024)}, u32[]{:S(2)}) copy-start(f32[1024]{0:T(1024)} %copy-done.11) | copy-start | bytes 12292
  1151.5 62.1 %copy-start.14 = (f32[1024]{0:T(1024)S(1)}, f32[1024]{0:T(1024)}, u32[]{:S(2)}) copy-start(f32[1024]{0:T(1024)} %param.20) | copy-start | bytes 12292
  1151.5 62.1 %copy-start.16 = (f32[1024]{0:T(1024)S(1)}, f32[1024]{0:T(1024)}, u32[]{:S(2)}) copy-start(f32[1024]{0:T(1024)} %param.22) | copy-start | bytes 12292
  1213.6 70.3 %copy-start.20 = (f32[1024]{0:T(1024)S(1)}, f32[1024]{0:T(1024)}, u32[]{:S(2)}) copy-start(f32[1024]{0:T(1024)} %param.31) | copy-start | bytes 12292
  1213.6 70.3 %copy-start.21 = (f32[1024]{0:T(1024)S(1)}, f32[1024]{0:T(1024)}, u32[]{:S(2)}) copy-start(f32[1024]{0:T(1024)} %param.27) | copy-start | bytes 12292
  1332.5 321.4 %copy-start.22 = (f32[1024]{0:T(1024)}, f32[1024]{0:T(1024)S(1)}, u32[]{:S(2)}) copy-start(f32[1024]{0:T(1024)S(1)} %get-tuple-element.552) | copy-start | bytes 12292
Sparse Core Ops, SparseCore 0:
  10.2 40.5 all-gather.11
  52.3 55.6 all-gather.19
  110.3 45.4 all-gather.9
  157.2 55.0 all-gather.7
  213.7 56.7 all-gather.13
  272.5 50.4 all-gather.15
  325.1 48.8 all-gather.17
  981.1 99.5 reduce-scatter.9
  1083.0 99.3 reduce-scatter.11
  1184.5 99.3 reduce-scatter.7
  1288.2 61.8 reduce-scatter.15
  1354.4 83.9 reduce-scatter.13
  1443.1 102.5 reduce-scatter.17
  1550.2 103.0 reduce-scatter.19
where the time goes:
time: 1670 us; the launch traced here: 1660 us
  matrix products  621 us (37%)
  waiting for transfers between devices  573 us (34%)
  other arithmetic  206 us (12%)
  local copies, waits for them, and re-layouts  138 us (8%)
  blocking collectives  101 us (6%)
    dot_general x8, matrix products, causal_scores(): jnp.einsum('qhd,khd->hqk', query_rows, key_rows, preferred_element_type=j...  158 us
    convert_element_type x4, other arithmetic, back_block(): score_grad = (attention * (prob_grad - jnp.sum(attention * prob_grad, axi...  110 us
    reduce_scatter x1, waiting for transfers between devices, body(): lax.psum_scatter(shrink_grad, 'fsdp', scatter_dimension=1, tiled=True)  108 us
    reduce_scatter x1, waiting for transfers between devices, body(): lax.psum_scatter(expand_grad, 'fsdp', scatter_dimension=0, tiled=True)  107 us
    reduce_scatter x1, waiting for transfers between devices, body(): lax.psum_scatter(project_grad, 'fsdp', scatter_dimension=0, tiled=True)  88.4 us
    dynamic_update_slice x8, local copies, waits for them, and re-layouts, back_sequence(): lax.scan(back_block, (zero_heads, zero_heads), (jnp.arange(block_count),...  88.3 us
    dot_general x4, matrix products, back_block(): jnp.einsum('qhd,khd->hqk', block_grads, seq_values, preferred_element_typ...  69.5 us
    dot_general x4, matrix products, back_block(): jnp.einsum('hqk,qhd->khd', attention.astype(jnp.bfloat16), block_grads, p...  66.8 us
  transfers between devices with their start and end apart: 14, of which 9 were waited for; matrix products, arithmetic and copies ran while one was open for 58% of the time, Pallas kernels for 0%

commit v1 on v0

--- a/solution.py
+++ b/solution.py
@@ -80,7 +80,10 @@
     shrink_bias,
 ):
     project_full, expand_full = (
-        lax.all_gather(project_weight, "fsdp", axis=0, tiled=True),
+        jnp.concatenate(
+            lax.all_to_all(jnp.stack([project_weight] * lax.axis_size("fsdp")), "fsdp", 0, 0),
+            axis=0,
+        ),
         lax.all_gather(expand_weight, "fsdp", axis=0, tiled=True),
     )
     dense_full, shrink_full = (

time: 1670 us -> 1650 us (0.988)
  waiting for transfers between devices: 573 us -> 556 us
    all_gather x1 -> x0, waiting for transfers between devices: 41.5 us -> none  [body(): lax.all_gather(project_weight, 'fsdp', axis=0, tiled=True)]
    all_gather x1, waiting for transfers between devices: 32.8 us -> 52.8 us  [body(): lax.all_gather(dense_weight, 'fsdp', axis=1, tiled=True)]
  transfers between devices with their start and end apart: 14 -> 14, of which waited for: 9 -> 8; matrix products, arithmetic and copies ran while one was open for 58% -> 58% of each run, Pallas kernels for 0% -> 0%
where the time goes in v1:
time: 1650 us; the launch traced here: 1640 us
  matrix products  624 us (38%)
  waiting for transfers between devices  556 us (34%)
  other arithmetic  202 us (12%)
  local copies, waits for them, and re-layouts  131 us (8%)
  blocking collectives  101 us (6%)
    dot_general x8, matrix products, causal_scores(): jnp.einsum('qhd,khd->hqk', query_rows, key_rows, preferred_element_type=j...  159 us
    convert_element_type x4, other arithmetic, back_block(): score_grad = (attention * (prob_grad - jnp.sum(attention * prob_grad, axi...  110 us
    reduce_scatter x1, waiting for transfers between devices, body(): lax.psum_scatter(shrink_grad, 'fsdp', scatter_dimension=1, tiled=True)  108 us
    reduce_scatter x1, waiting for transfers between devices, body(): lax.psum_scatter(expand_grad, 'fsdp', scatter_dimension=0, tiled=True)  107 us
    reduce_scatter x1, waiting for transfers between devices, body(): lax.psum_scatter(project_grad, 'fsdp', scatter_dimension=0, tiled=True)  88.6 us
    dynamic_update_slice x8, local copies, waits for them, and re-layouts, back_sequence(): lax.scan(back_block, (zero_heads, zero_heads), (jnp.arange(block_count),...  88.4 us
    reduce_scatter x1, waiting for transfers between devices, body(): lax.psum_scatter(jnp.dot(context, dense_full, preferred_element_type=jnp....  73.4 us
    dot_general x4, matrix products, back_block(): jnp.einsum('qhd,khd->hqk', block_grads, seq_values, preferred_element_typ...  69.5 us
  transfers between devices with their start and end apart: 14, of which 8 were waited for; matrix products, arithmetic and copies ran while one was open for 58% of the time, Pallas kernels for 0%

profile of v1, /device:TPU:0, one launch (start us, length us, event | category | flops | bytes accessed | tf_op | source)
XLA Modules:
  0.0 1644.6 jit_solution(14907341609069775003)
XLA Ops:
  26.8 52.8 %all-gather.9.cloned.1.call-done = bf16[512,1024]{0,1:T(8,128)(2,1)} async-done(((bf16[512,64]{0,1:T(8,128)(2,1)}), bf16[512,1024]{0,1:T(8,128)(2,1)}) %all-gather.9.cloned.1.call-update) | async-done | bytes 1048592 | tf_op jit(solution)/shard_map/all_gather | solution.py:90
  79.6 60.4 %all-gather.17.cloned.1.call-done = bf16[2048,1024]{1,0:T(8,128)(2,1)} async-done(((bf16[1024,1024]{1,0:T(8,128)(2,1)}), bf16[2048,1024]{1,0:T(8,128)(2,1)}) %all-gather.17.cloned.1.call-update) | async-done | bytes 4194320 | tf_op jit(solution)/shard_map/all_gather | solution.py:157
  153.4 44.9 %all-gather.7.cloned.1.call-done = bf16[2048,1024]{1,0:T(8,128)(2,1)} async-done(((bf16[1024,1024]{1,0:T(8,128)(2,1)}), bf16[2048,1024]{1,0:T(8,128)(2,1)}) %all-gather.7.cloned.1.call-update) | async-done | bytes 4194320 | tf_op jit(solution)/shard_map/all_gather | solution.py:101
  221.3 191.5 %while.49 = (s32[]{:T(128)}, bf16[4,512,8,64]{1,3,2,0:T(8,128)(2,1)}, f32[4,8,512]{2,1,0:T(8,128)S(1)}, s32[4]{0:T(128)S(1)}, bf16[2048,8,64]{0,2,1:T(8,128)(2,1...) while((s32[]{:T(128)}, ...), condition=%wide.region_5.6_spmd, body=%wide.region_2.5_spmd.sunk | while | flops 2249454080 | bytes 110236336 | solution.py:143
  223.7 14.9 fusion.121
  238.5 15.0 fusion.122
  253.5 15.6 fusion.123
  271.1 15.4 fusion.121
  286.4 15.2 fusion.122
  301.6 15.7 fusion.123
  319.2 14.9 fusion.121
  334.1 15.4 fusion.122
  349.5 15.9 fusion.123
  367.4 14.9 fusion.121
  382.2 15.0 fusion.122
  397.2 15.5 fusion.123
  412.8 524.1 %while.50 = (s32[]{:T(128)}, f32[2048,8,64]{0,2,1:T(8,128)}, f32[2048,8,64]{0,2,1:T(8,128)}, f32[4,512,8,64]{1,0,3,2:T(4,128)}, s32[4]{0:T(128)S(1)}, /*index=5*...) while((s32[]{:T(128)}, f32[2048,8,64]{0,2,1:T(8,128)}, ...), condition=%wide.region_9.10_spmd.clone, body=%wide.region_7.9_spmd.clone.sunk | while | flops 5450756608 | bytes 284250304 | solution.py:213
  414.2 17.4 %fusion.133 = f32[8,512,2048]{2,1,0:T(8,128)} fusion(bf16[2048,8,64]{0,2,1:T(8,128)(2,1)} %get-tuple-element.520, bf16[2048,8,64]{0,2,1:T(8,128)(2,1)} %get-tuple-element.519, s32[]{:T(128)S(6)} %select_n.101), kind=kOutput, calls=%fused_computation.28.clone.1 | convolution fusion | flops 1073741824 | bytes 36175876 | tf_op jit(solution)/shard_map/while/body/eval_jaxpr/while/body/eval_jaxpr/qhd,khd->hqk/dot_general | solution.py:187
  432.3 24.7 %multiply_reduce_fusion.4 = (f32[8,512]{1,0:T(8,128)S(1)}, f32[8,512,2048]{2,1,0:T(8,128)}) fusion(f32[8,512,2048]{2,1,0:T(8,128)} %fusion.133, f32[8,512]{1,0:T(8,128)S(1)} %dynamic-slice_bitcast_fusion.2, bf16[2048,8,64]{0,2,1:T(8,128)(2,1)S(1)} %get-tuple-element.517, bf16[2048,8,64]{0,2,1:T(8,128)(2,1)} %get-tuple-element.516, ...), kind=kOutput, calls=%fused_computation.18.clone.1 | convolution fusion | flops 1115680768 | bytes 70811648 | tf_op jit(solution)/shard_map/while/body/eval_jaxpr/while/body/eval_jaxpr/qhd,khd->hqk/dot_general | solution.py:54
  457.0 27.4 %multiply_convert_fusion.3 = bf16[8,512,2048]{2,1,0:T(8,128)(2,1)} fusion(f32[8,512,2048]{2,1,0:T(8,128)} %get-tuple-element.448, f32[8,512,2048]{2,1,0:T(8,128)} %fusion.133, f32[8,512]{1,0:T(8,128)S(1)} %get-tuple-element.449), kind=kLoop, calls=%fused_computation.17.clone.1 | loop fusion | flops 25165824 | bytes 83902464 | tf_op jit(solution)/shard_map/while/body/eval_jaxpr/while/body/eval_jaxpr/convert_element_type | solution.py:192
  494.2 21.0 %dynamic_update_slice.39 = f32[4,512,8,64]{1,0,3,2:T(4,128)} dynamic-update-slice(f32[4,512,8,64]{1,0,3,2:T(4,128)} %get-tuple-element.500, f32[1,512,8,64]{1,0,3,2:T(1,128)S(1)} %copy.60, s32[]{:T(128)} %get-tuple-element.497, s32[]{:T(128)} %constant.176.clone.1..sunk.1, s32[]{:T(128)} %constant.176.clone.1..sunk.1, s32[]{:T(128)} %constant.176.clone.1..sunk.1) | dynamic-update-slice | bytes 2097156 | tf_op jit(solution)/shard_map/while/body/eval_jaxpr/while/body/jit(dynamic_update_index_in_dim)/dynamic_update_slice | solution.py:213
  526.3 15.8 bitcast_add_fusion.5
  543.3 17.4 %fusion.133 = f32[8,512,2048]{2,1,0:T(8,128)} fusion(bf16[2048,8,64]{0,2,1:T(8,128)(2,1)} %get-tuple-element.520, bf16[2048,8,64]{0,2,1:T(8,128)(2,1)} %get-tuple-element.519, s32[]{:T(128)S(6)} %select_n.101), kind=kOutput, calls=%fused_computation.28.clone.1 | convolution fusion | flops 1073741824 | bytes 36175876 | tf_op jit(solution)/shard_map/while/body/eval_jaxpr/while/body/eval_jaxpr/qhd,khd->hqk/dot_general | solution.py:187
  561.4 24.7 %multiply_reduce_fusion.4 = (f32[8,512]{1,0:T(8,128)S(1)}, f32[8,512,2048]{2,1,0:T(8,128)}) fusion(f32[8,512,2048]{2,1,0:T(8,128)} %fusion.133, f32[8,512]{1,0:T(8,128)S(1)} %dynamic-slice_bitcast_fusion.2, bf16[2048,8,64]{0,2,1:T(8,128)(2,1)S(1)} %get-tuple-element.517, bf16[2048,8,64]{0,2,1:T(8,128)(2,1)} %get-tuple-element.516, ...), kind=kOutput, calls=%fused_computation.18.clone.1 | convolution fusion | flops 1115680768 | bytes 70811648 | tf_op jit(solution)/shard_map/while/body/eval_jaxpr/while/body/eval_jaxpr/qhd,khd->hqk/dot_general | solution.py:54
  586.1 27.4 %multiply_convert_fusion.3 = bf16[8,512,2048]{2,1,0:T(8,128)(2,1)} fusion(f32[8,512,2048]{2,1,0:T(8,128)} %get-tuple-element.448, f32[8,512,2048]{2,1,0:T(8,128)} %fusion.133, f32[8,512]{1,0:T(8,128)S(1)} %get-tuple-element.449), kind=kLoop, calls=%fused_computation.17.clone.1 | loop fusion | flops 25165824 | bytes 83902464 | tf_op jit(solution)/shard_map/while/body/eval_jaxpr/while/body/eval_jaxpr/convert_element_type | solution.py:192
  623.3 21.0 %dynamic_update_slice.39 = f32[4,512,8,64]{1,0,3,2:T(4,128)} dynamic-update-slice(f32[4,512,8,64]{1,0,3,2:T(4,128)} %get-tuple-element.500, f32[1,512,8,64]{1,0,3,2:T(1,128)S(1)} %copy.60, s32[]{:T(128)} %get-tuple-element.497, s32[]{:T(128)} %constant.176.clone.1..sunk.1, s32[]{:T(128)} %constant.176.clone.1..sunk.1, s32[]{:T(128)} %constant.176.clone.1..sunk.1) | dynamic-update-slice | bytes 2097156 | tf_op jit(solution)/shard_map/while/body/eval_jaxpr/while/body/jit(dynamic_update_index_in_dim)/dynamic_update_slice | solution.py:213
  656.6 17.0 %bitcast_add_fusion.5 = f32[2048,8,64]{0,2,1:T(8,128)} fusion(f32[2048,8,64]{0,2,1:T(8,128)} %get-tuple-element.499, f32[8,512,2048]{2,1,0:T(8,128)} %get-tuple-element.448, pred[]{:T(512)S(6)} %compare.4, bf16[2048,8,64]{0,2,1:T(8,128)(2,1)} %get-tuple-element.519, s32[]{:T(128)S(6)} %select_n.101), kind=kOutput, calls=%fused_computation.22.clone.1 | convolution fusion | flops 1084227584 | bytes 42467332 | tf_op jit(solution)/shard_map/while/body/eval_jaxpr/while/body/eval_jaxpr/hqk,qhd->khd/dot_general | solution.py:204
  674.8 17.4 %fusion.133 = f32[8,512,2048]{2,1,0:T(8,128)} fusion(bf16[2048,8,64]{0,2,1:T(8,128)(2,1)} %get-tuple-element.520, bf16[2048,8,64]{0,2,1:T(8,128)(2,1)} %get-tuple-element.519, s32[]{:T(128)S(6)} %select_n.101), kind=kOutput, calls=%fused_computation.28.clone.1 | convolution fusion | flops 1073741824 | bytes 36175876 | tf_op jit(solution)/shard_map/while/body/eval_jaxpr/while/body/eval_jaxpr/qhd,khd->hqk/dot_general | solution.py:187
  692.9 24.7 %multiply_reduce_fusion.4 = (f32[8,512]{1,0:T(8,128)S(1)}, f32[8,512,2048]{2,1,0:T(8,128)}) fusion(f32[8,512,2048]{2,1,0:T(8,128)} %fusion.133, f32[8,512]{1,0:T(8,128)S(1)} %dynamic-slice_bitcast_fusion.2, bf16[2048,8,64]{0,2,1:T(8,128)(2,1)S(1)} %get-tuple-element.517, bf16[2048,8,64]{0,2,1:T(8,128)(2,1)} %get-tuple-element.516, ...), kind=kOutput, calls=%fused_computation.18.clone.1 | convolution fusion | flops 1115680768 | bytes 70811648 | tf_op jit(solution)/shard_map/while/body/eval_jaxpr/while/body/eval_jaxpr/qhd,khd->hqk/dot_general | solution.py:54
  717.6 27.4 %multiply_convert_fusion.3 = bf16[8,512,2048]{2,1,0:T(8,128)(2,1)} fusion(f32[8,512,2048]{2,1,0:T(8,128)} %get-tuple-element.448, f32[8,512,2048]{2,1,0:T(8,128)} %fusion.133, f32[8,512]{1,0:T(8,128)S(1)} %get-tuple-element.449), kind=kLoop, calls=%fused_computation.17.clone.1 | loop fusion | flops 25165824 | bytes 83902464 | tf_op jit(solution)/shard_map/while/body/eval_jaxpr/while/body/eval_jaxpr/convert_element_type | solution.py:192
  754.8 21.0 %dynamic_update_slice.39 = f32[4,512,8,64]{1,0,3,2:T(4,128)} dynamic-update-slice(f32[4,512,8,64]{1,0,3,2:T(4,128)} %get-tuple-element.500, f32[1,512,8,64]{1,0,3,2:T(1,128)S(1)} %copy.60, s32[]{:T(128)} %get-tuple-element.497, s32[]{:T(128)} %constant.176.clone.1..sunk.1, s32[]{:T(128)} %constant.176.clone.1..sunk.1, s32[]{:T(128)} %constant.176.clone.1..sunk.1) | dynamic-update-slice | bytes 2097156 | tf_op jit(solution)/shard_map/while/body/eval_jaxpr/while/body/jit(dynamic_update_index_in_dim)/dynamic_update_slice | solution.py:213
  788.0 17.0 %bitcast_add_fusion.5 = f32[2048,8,64]{0,2,1:T(8,128)} fusion(f32[2048,8,64]{0,2,1:T(8,128)} %get-tuple-element.499, f32[8,512,2048]{2,1,0:T(8,128)} %get-tuple-element.448, pred[]{:T(512)S(6)} %compare.4, bf16[2048,8,64]{0,2,1:T(8,128)(2,1)} %get-tuple-element.519, s32[]{:T(128)S(6)} %select_n.101), kind=kOutput, calls=%fused_computation.22.clone.1 | convolution fusion | flops 1084227584 | bytes 42467332 | tf_op jit(solution)/shard_map/while/body/eval_jaxpr/while/body/eval_jaxpr/hqk,qhd->khd/dot_general | solution.py:204
  806.3 17.4 %fusion.133 = f32[8,512,2048]{2,1,0:T(8,128)} fusion(bf16[2048,8,64]{0,2,1:T(8,128)(2,1)} %get-tuple-element.520, bf16[2048,8,64]{0,2,1:T(8,128)(2,1)} %get-tuple-element.519, s32[]{:T(128)S(6)} %select_n.101), kind=kOutput, calls=%fused_computation.28.clone.1 | convolution fusion | flops 1073741824 | bytes 36175876 | tf_op jit(solution)/shard_map/while/body/eval_jaxpr/while/body/eval_jaxpr/qhd,khd->hqk/dot_general | solution.py:187
  824.3 24.7 %multiply_reduce_fusion.4 = (f32[8,512]{1,0:T(8,128)S(1)}, f32[8,512,2048]{2,1,0:T(8,128)}) fusion(f32[8,512,2048]{2,1,0:T(8,128)} %fusion.133, f32[8,512]{1,0:T(8,128)S(1)} %dynamic-slice_bitcast_fusion.2, bf16[2048,8,64]{0,2,1:T(8,128)(2,1)S(1)} %get-tuple-element.517, bf16[2048,8,64]{0,2,1:T(8,128)(2,1)} %get-tuple-element.516, ...), kind=kOutput, calls=%fused_computation.18.clone.1 | convolution fusion | flops 1115680768 | bytes 70811648 | tf_op jit(solution)/shard_map/while/body/eval_jaxpr/while/body/eval_jaxpr/qhd,khd->hqk/dot_general | solution.py:54
  849.1 27.4 %multiply_convert_fusion.3 = bf16[8,512,2048]{2,1,0:T(8,128)(2,1)} fusion(f32[8,512,2048]{2,1,0:T(8,128)} %get-tuple-element.448, f32[8,512,2048]{2,1,0:T(8,128)} %fusion.133, f32[8,512]{1,0:T(8,128)S(1)} %get-tuple-element.449), kind=kLoop, calls=%fused_computation.17.clone.1 | loop fusion | flops 25165824 | bytes 83902464 | tf_op jit(solution)/shard_map/while/body/eval_jaxpr/while/body/eval_jaxpr/convert_element_type | solution.py:192
  886.3 21.0 %dynamic_update_slice.39 = f32[4,512,8,64]{1,0,3,2:T(4,128)} dynamic-update-slice(f32[4,512,8,64]{1,0,3,2:T(4,128)} %get-tuple-element.500, f32[1,512,8,64]{1,0,3,2:T(1,128)S(1)} %copy.60, s32[]{:T(128)} %get-tuple-element.497, s32[]{:T(128)} %constant.176.clone.1..sunk.1, s32[]{:T(128)} %constant.176.clone.1..sunk.1, s32[]{:T(128)} %constant.176.clone.1..sunk.1) | dynamic-update-slice | bytes 2097156 | tf_op jit(solution)/shard_map/while/body/eval_jaxpr/while/body/jit(dynamic_update_index_in_dim)/dynamic_update_slice | solution.py:213
  919.5 17.0 %bitcast_add_fusion.5 = f32[2048,8,64]{0,2,1:T(8,128)} fusion(f32[2048,8,64]{0,2,1:T(8,128)} %get-tuple-element.499, f32[8,512,2048]{2,1,0:T(8,128)} %get-tuple-element.448, pred[]{:T(512)S(6)} %compare.4, bf16[2048,8,64]{0,2,1:T(8,128)(2,1)} %get-tuple-element.519, s32[]{:T(128)S(6)} %select_n.101), kind=kOutput, calls=%fused_computation.22.clone.1 | convolution fusion | flops 1084227584 | bytes 42467332 | tf_op jit(solution)/shard_map/while/body/eval_jaxpr/while/body/eval_jaxpr/hqk,qhd->khd/dot_general | solution.py:204
  965.7 49.3 %multiply_convert_fusion.1 = (bf16[2048,2048]{1,0:T(8,128)(2,1)}, f32[2048,2048]{1,0:T(8,128)}, f32[2048,2048]{1,0:T(8,128)}) fusion(f32[2048]{0:T(1024)S(1)} %copy-done.28, bf16[2048,1024]{1,0:T(8,128)(2,1)} %all-gather.11.cloned.1.call-done, bf16[1024,2048]{1,0:T(8,128)(2,1)} %all-gather.13.cloned.1.call-done), kind=kOutput, calls=%fused_computation.42 | convolution fusion | flops 8866758656 | bytes 50339840 | tf_op jit(solution)/shard_map/dot_general | solution.py:147
  1015.0 27.8 %convert_reduce_fusion = (f32[2048]{0:T(1024)S(1)}, bf16[2048,2048]{1,0:T(8,128)(2,1)}) fusion(f32[2048,2048]{1,0:T(8,128)} %get-tuple-element.306, bf16[2048,1024]{1,0:T(8,128)(2,1)} %all-gather.17.cloned.1.call-done, bf16[2048,1024]{0,1:T(8,128)(2,1)} %all-gather.15.cloned.1.call-done, f32[2048,2048]{1,0:T(8,128)} %get-tuple-element.333, ...), kind=kOutput, calls=%fused_computation.40 | convolution fusion | flops 8661235712 | bytes 50348032 | tf_op jit(solution)/shard_map/dot_general | solution.py:163
  1096.7 15.0 fusion.73
  1111.9 14.7 fusion.74
  1127.3 61.1 %all-reduce.1 = (f32[3,512]{1,0:T(4,128)}, f32[2048]{0:T(1024)}) all-reduce(f32[3,512]{1,0:T(4,128)S(1)} %copy-done.20, f32[2048]{0:T(1024)S(1)} %get-tuple-element.334), channel_id=1, replica_groups=mesh['fsdp'=16,'tp'=2] {'fsdp'}, use_global_device_ids=true, to_apply=%region_26.27 | all-reduce | flops 3584 | bytes 28672 | tf_op jit(solution)/shard_map/psum | solution.py:255
  1194.4 73.4 %reduce-scatter.8.cloned.1.call-done = f32[1024,1024]{1,0:T(8,128)} async-done(((f32[2048,1024]{1,0:T(8,128)}), f32[1024,1024]{1,0:T(8,128)}) %reduce-scatter.8.cloned.1.call-update) | async-done | bytes 4194320 | tf_op jit(solution)/shard_map/reduce_scatter | solution.py:149
  1276.4 39.9 %all-reduce = (f32[1024]{0:T(1024)}, f32[1024]{0:T(1024)}, f32[1024]{0:T(1024)}, f32[1024]{0:T(1024)}, f32[1024]{0:T(1024)S(1)}) all-reduce(f32[1024]{0:T(1024)S(1)} %get-tuple-element.252, f32[1024]{0:T(1024)S(1)} %get-tuple-element.257, f32[1024]{0:T(1024)S(1)} %get-tuple-element.261, ...), channel_id=1, replica_groups=mesh['fsdp'=16,'tp'=2] {'fsdp','tp'}, use_global_device_ids=true, to_apply=%region_17.18 | all-reduce | flops 5120 | bytes 40960 | tf_op jit(solution)/shard_map/psum | solution.py:250
  1316.3 17.6 %reduce-scatter.16.cloned.1.call-done = f32[512,64]{0,1:T(8,128)} async-done(((f32[512,1024]{0,1:T(8,128)}), f32[512,64]{0,1:T(8,128)}) %reduce-scatter.16.cloned.1.call-update) | async-done | bytes 131088 | tf_op jit(solution)/shard_map/reduce_scatter | solution.py:261
  1333.9 88.6 %reduce-scatter.14.cloned.1.call-done = f32[64,3,512]{2,0,1:T(8,128)} async-done(((f32[1024,3,512]{2,0,1:T(8,128)}), f32[64,3,512]{2,0,1:T(8,128)}) %reduce-scatter.14.cloned.1.call-update) | async-done | bytes 393232 | tf_op jit(solution)/shard_map/reduce_scatter | solution.py:257
  1422.4 107.2 %reduce-scatter.18.cloned.1.call-done = f32[64,2048]{1,0:T(8,128)} async-done(((f32[1024,2048]{1,0:T(8,128)}), f32[64,2048]{1,0:T(8,128)}) %reduce-scatter.18.cloned.1.call-update) | async-done | bytes 524304 | tf_op jit(solution)/shard_map/reduce_scatter | solution.py:258
  1529.6 107.7 %reduce-scatter.20.cloned.1.call-done = f32[2048,64]{0,1:T(8,128)} async-done(((f32[2048,1024]{0,1:T(8,128)}), f32[2048,64]{0,1:T(8,128)}) %reduce-scatter.20.cloned.1.call-update) | async-done | bytes 524304 | tf_op jit(solution)/shard_map/reduce_scatter | solution.py:262
  (184 shorter events, 250.9 us)
Async XLA Ops:
  7.2 3.5 copy-start.1
  7.2 4.2 copy-start.16
  7.2 4.2 copy-start.21
  7.2 4.2 copy-start.18
  7.2 4.2 copy-start.22
  7.2 72.4 %all-gather.9.cloned.1.call-start = ((), (), s32[]{:S(2)}) async-start(), calls=%async_computation.9 | async-start | bytes 1114112 | tf_op jit(solution)/shard_map/all_gather | solution.py:90
  8.0 132.1 %all-gather.17.cloned.1.call-start = ((), (), s32[]{:S(2)}) async-start(), calls=%async_computation.14 | async-start | bytes 6291456 | tf_op jit(solution)/shard_map/all_gather | solution.py:157
  8.7 189.6 %all-gather.7.cloned.1.call-start = ((), (), s32[]{:S(2)}) async-start(), calls=%async_computation.8 | async-start | bytes 6291456 | tf_op jit(solution)/shard_map/all_gather | solution.py:101
  10.7 3.6 copy-start.12
  11.5 2.8 copy-start.14
  11.5 4.0 copy-start.11
  14.3 950.8 %all-gather.11.cloned.1.call-start = ((), (), s32[]{:S(2)}) async-start(), calls=%async_computation.10 | async-start | bytes 6291456 | tf_op jit(solution)/shard_map/all_gather | solution.py:102
  14.9 950.3 %all-gather.13.cloned.1.call-start = ((), (), s32[]{:S(2)}) async-start(), calls=%async_computation.11 | async-start | bytes 4456448 | tf_op jit(solution)/shard_map/all_gather | solution.py:87
  17.5 128.7 %all-to-all-start = ((bf16[16,64,3,512]{3,1,2,0:T(8,128)(2,1)}), bf16[16,64,3,512]{3,1,2,0:T(8,128)(2,1)S(1)}, u32[]{:S(2)}, u32[]{:S(2)}) async-start(bf16[16,64,3,512]{3,1,2,0:T(8,128)(2,1)} %stack.4), calls=%async_computation | async-start | bytes 6291456 | tf_op jit(solution)/shard_map/all_to_all | solution.py:84
  24.9 990.1 %all-gather.15.cloned.1.call-start = ((), (), s32[]{:S(2)}) async-start(), calls=%async_computation.12 | async-start | bytes 4456448 | tf_op jit(solution)/shard_map/all_gather | solution.py:91
  25.5 1163.0 %reduce-scatter.10.cloned.1.call-start = ((), (), s32[]{:S(2)}) async-start(), calls=%async_computation.15 | async-start | bytes 12582912 | tf_op jit(solution)/shard_map/reduce_scatter | solution.py:236
  26.8 192.6 %copy-start.8 = (f32[2048,8]{0,1:T(8,128)}, f32[2048,8]{0,1:T(8,128)S(1)}, u32[]{:S(2)}) copy-start(f32[2048,8]{0,1:T(8,128)S(1)} %get-tuple-element.332) | copy-start | bytes 196612
  150.0 60.6 %copy-start.3 = (bf16[128,8,3,512]{3,1,2,0:T(8,128)(2,1)}, bf16[128,8,3,512]{3,1,2,0:T(8,128)(2,1)S(1)}, u32[]{:S(2)}) copy-start(bf16[128,8,3,512]{3,1,2,0:T(8,128)(2,1)S(1)} %copy.57) | copy-start | bytes 9437188
  150.0 48.3 %copy-start.27 = (f32[3,512]{1,0:T(4,128)S(1)}, f32[3,512]{1,0:T(4,128)}, u32[]{:S(2)}) copy-start(f32[3,512]{1,0:T(4,128)} %param.25) | copy-start | bytes 18436
  943.0 4.3 copy-start.9
  943.0 4.3 copy-start.10
  949.1 2.2 copy-start
  951.3 4.5 copy-start.4
  953.1 2.7 copy-start.5
  965.0 0.7 copy-start.28
  965.1 223.4 %reduce-scatter.12.cloned.1.call-start = ((), (), s32[]{:S(2)}) async-start(), calls=%async_computation.16 | async-start | bytes 12582912 | tf_op jit(solution)/shard_map/reduce_scatter | solution.py:237
  1057.3 1.6 copy-start.6
  1057.4 210.5 %reduce-scatter.8.cloned.1.call-start = ((), (), s32[]{:S(2)}) async-start(), calls=%async_computation.13 | async-start | bytes 12582912 | tf_op jit(solution)/shard_map/reduce_scatter | solution.py:149
  1058.9 2.3 copy-start.26
  1061.2 11.4 copy-start.7
  1078.2 255.6 %reduce-scatter.16.cloned.1.call-start = ((), (), s32[]{:S(2)}) async-start(), calls=%async_computation.18 | async-start | bytes 2228224 | tf_op jit(solution)/shard_map/reduce_scatter | solution.py:261
  1084.2 338.2 %reduce-scatter.14.cloned.1.call-start = ((), (), s32[]{:S(2)}) async-start(), calls=%async_computation.17 | async-start | bytes 6684672 | tf_op jit(solution)/shard_map/reduce_scatter | solution.py:257
  1096.7 432.9 %reduce-scatter.18.cloned.1.call-start = ((), (), s32[]{:S(2)}) async-start(), calls=%async_computation.19 | async-start | bytes 8912896 | tf_op jit(solution)/shard_map/reduce_scatter | solution.py:258
  1111.7 525.6 %reduce-scatter.20.cloned.1.call-start = ((), (), s32[]{:S(2)}) async-start(), calls=%async_computation.20 | async-start | bytes 8912896 | tf_op jit(solution)/shard_map/reduce_scatter | solution.py:262
  1126.6 0.7 copy-start.20
  1126.6 61.9 %copy-start.2 = (bf16[1024,1024]{1,0:T(8,128)(2,1)S(1)}, bf16[1024,1024]{1,0:T(8,128)(2,1)}, u32[]{:S(2)}) copy-start(bf16[1024,1024]{1,0:T(8,128)(2,1)} %param.18) | copy-start | bytes 6291460
  1126.6 61.9 %copy-start.13 = (f32[1024]{0:T(1024)S(1)}, f32[1024]{0:T(1024)}, u32[]{:S(2)}) copy-start(f32[1024]{0:T(1024)} %copy-done.12) | copy-start | bytes 12292
  1126.6 61.9 %copy-start.15 = (f32[1024]{0:T(1024)S(1)}, f32[1024]{0:T(1024)}, u32[]{:S(2)}) copy-start(f32[1024]{0:T(1024)} %copy-done.14) | copy-start | bytes 12292
  1126.6 61.9 %copy-start.17 = (f32[1024]{0:T(1024)S(1)}, f32[1024]{0:T(1024)}, u32[]{:S(2)}) copy-start(f32[1024]{0:T(1024)} %param.20) | copy-start | bytes 12292
  1126.6 61.9 %copy-start.19 = (f32[1024]{0:T(1024)S(1)}, f32[1024]{0:T(1024)}, u32[]{:S(2)}) copy-start(f32[1024]{0:T(1024)} %param.22) | copy-start | bytes 12292
  1188.5 79.4 %copy-start.23 = (f32[1024]{0:T(1024)S(1)}, f32[1024]{0:T(1024)}, u32[]{:S(2)}) copy-start(f32[1024]{0:T(1024)} %param.31) | copy-start | bytes 12292
  1188.5 79.4 %copy-start.24 = (f32[1024]{0:T(1024)S(1)}, f32[1024]{0:T(1024)}, u32[]{:S(2)}) copy-start(f32[1024]{0:T(1024)} %param.27) | copy-start | bytes 12292
  1316.3 321.6 %copy-start.25 = (f32[1024]{0:T(1024)}, f32[1024]{0:T(1024)S(1)}, u32[]{:S(2)}) copy-start(f32[1024]{0:T(1024)S(1)} %get-tuple-element.552) | copy-start | bytes 12292
Sparse Core Ops, SparseCore 0:
  10.2 69.3 all-gather.8
  81.2 58.8 all-gather.16
  141.6 56.7 all-gather.6
  199.7 56.7 all-gather.10
  258.5 50.2 all-gather.12
  310.8 48.8 all-gather.14
  965.2 99.2 reduce-scatter.9
  1066.8 99.3 reduce-scatter.11
  1168.5 99.3 reduce-scatter.7
  1272.0 61.8 reduce-scatter.15
  1338.4 83.9 reduce-scatter.13
  1426.9 102.6 reduce-scatter.17
  1534.2 103.0 reduce-scatter.19
